TPU v7x, 32 devices: a whole 2x2x4 slice. The times are simulated.
32 devices in a mesh: task: 8 (over z, y), aux: 4 (over x, core).
Axes of the slice: x: 2, y: 2, z: 4, core: 2. Of those that a mesh axis runs over, the one named last changes fastest.
Arguments:
- factors: bfloat16 [8, 2048, 1024], P('task', 'aux'), may hold values from -0.125 to 0.125
- amplitudes: bfloat16 [8, 256, 1024], P('task'), may hold values from -6 to 6
- task_counts: int32 [8], P('task'), may hold values from 1 to 4, 16 in all
- task_tiles: int32 [8, 4, 3], P('task'), may hold values from 0 to 4
Outputs:
- residual: float32 [8, 256, 1024], P('task', None, 'aux')
Inputs may be any that keep to these rules, and one draw needn't show every extreme that they name: `task_counts`: every tile has 1 to 4 tasks, exactly 16 in all; some tile has exactly 4.
All inputs are finite; a program needn't handle non-finite values. No bound on the sum of `task_counts` on one device may be relied on, other than what follows from the above.
Results may differ from a plain program's by a relative error of at most 0.0026.
Values may be sent and summed in bfloat16 or wider, within the bound.
A program may use at most 64 MiB of HBM per device.

v0:
```python
import jax
import jax.numpy as jnp
from jax import lax
from jax.sharding import PartitionSpec as P

VB = 32
RADIUS = 2


def shifted(block, axis, distance):
    devices = range(lax.axis_size(axis))
    route = [((i - distance) % len(devices), i) for i in devices]
    return lax.ppermute(block, axis, route)


def task_term(first, second, amp, width):
    tile = lax.dot_general(
        first, second, (((0,), (0,)), ((), ())), preferred_element_type=jnp.float32
    )
    tile = (
        tile.reshape(width, width, width, width)
        .transpose(1, 3, 0, 2)
        .reshape(width * width, width * width)
    )
    tile = tile.astype(jnp.bfloat16)
    return jnp.dot(amp, tile, preferred_element_type=jnp.float32)


def run_tasks(window_fac, window_amp, plan, first, last, centre, lowest, width):

    def one_task(slot, total):
        offs = lax.dynamic_index_in_dim(plan, slot, 0, False) - RADIUS + centre - lowest
        left = lax.dynamic_index_in_dim(window_fac, offs[0], 0, False)
        right = lax.dynamic_index_in_dim(window_fac, offs[1], 0, False)
        amp = lax.dynamic_index_in_dim(window_amp, offs[2], 0, False)
        return total + task_term(left, right, amp, width)

    start = jnp.zeros((window_amp.shape[1], window_amp.shape[2]), jnp.float32)
    return lax.fori_loop(first, last, one_task, start)


def shards(factors, amplitudes, task_counts, task_tiles):
    width = VB
    own_fac = factors[0]
    own_amp = amplitudes[0]
    fac_list = []
    amp_list = []
    for offset in range(-RADIUS, RADIUS + 1):
        if offset == 0:
            fac_list.append(own_fac)
            amp_list.append(own_amp)
        else:
            moved = shifted((own_fac, own_amp), "task", -offset)
            fac_list.append(moved[0])
            amp_list.append(moved[1])
    window_fac = jnp.stack(fac_list)
    window_amp = jnp.stack(amp_list)
    partial_sum = run_tasks(
        window_fac, window_amp, task_tiles[0], 0, task_counts[0], 0, -RADIUS, width
    )
    summed = lax.psum_scatter(partial_sum, "aux", scatter_dimension=1, tiled=True)
    return summed[None]


def solution(mesh):
    return jax.shard_map(
        shards,
        mesh=mesh,
        in_specs=(P("task", "aux", None), P("task", None, None), P("task"), P("task", None, None)),
        out_specs=P("task", None, "aux"),
        check_vma=False,
    )
```

profile of v0, /device:TPU:0, one launch (start us, length us, event | category | flops | bytes accessed | tf_op | source)
XLA Modules:
  0.0 261.9 jit_solution(11815704583886749295)
XLA Ops:
  6.5 0.0 copy-start.3
  6.5 0.0 reduce-scatter.2.cloned.1.call-start
  6.5 3.1 %collective-permute-start = (bf16[256,1024]{1,0:T(8,128)(2,1)}, bf16[256,1024]{1,0:T(8,128)(2,1)}, u32[]{:S(2)}, u32[]{:S(2)}) collective-permute-start(bf16[256,1024]{1,0:T(8,128)(2,1)} %bitcast.78), channel_id=1, source_target_pairs={{24,0},{28,4},{0,8},{4,12},{8,16},{12,20},{16,24},{20,28},{25,1},{... | collective-permute-start | bytes 1572872 | tf_op jit(solution)/shard_map/ppermute | solution.py:13
  9.6 1.5 collective-permute-start.1
  11.1 2.2 collective-permute-start.3
  13.4 1.2 collective-permute-start.2
  14.6 1.5 copy.6
  16.1 2.0 collective-permute-start.7
  18.1 0.8 copy.5
  18.9 5.9 %collective-permute-done = bf16[256,1024]{1,0:T(8,128)(2,1)} collective-permute-done((bf16[256,1024]{1,0:T(8,128)(2,1)}, bf16[256,1024]{1,0:T(8,128)(2,1)}, u32[]{:S(2)}, u32[]{:S(2)}) %collective-permute-start) | collective-permute-done | bytes 524320 | tf_op jit(solution)/shard_map/ppermute | solution.py:13
  24.8 0.0 collective-permute-start.4
  24.8 1.1 bitcast_dynamic-update-slice_fusion.7
  25.9 11.3 %collective-permute-done.1 = bf16[256,1024]{1,0:T(8,128)(2,1)} collective-permute-done((bf16[256,1024]{1,0:T(8,128)(2,1)}, bf16[256,1024]{1,0:T(8,128)(2,1)}, u32[]{:S(2)}, u32[]{:S(2)}) %collective-permute-start.1) | collective-permute-done | bytes 524320 | tf_op jit(solution)/shard_map/ppermute | solution.py:13
  37.2 0.0 collective-permute-start.5
  37.2 1.1 bitcast_dynamic-update-slice_fusion.6
  38.2 0.0 copy-done.3
  38.3 6.4 %collective-permute-done.2 = bf16[256,1024]{1,0:T(8,128)(2,1)} collective-permute-done((bf16[256,1024]{1,0:T(8,128)(2,1)}, bf16[256,1024]{1,0:T(8,128)(2,1)}, u32[]{:S(2)}, u32[]{:S(2)}) %collective-permute-start.2) | collective-permute-done | bytes 524320 | tf_op jit(solution)/shard_map/ppermute | solution.py:13
  44.7 5.3 %collective-permute-start.6 = (bf16[512,1024]{0,1:T(8,128)(2,1)S(1)}, bf16[512,1024]{0,1:T(8,128)(2,1)S(1)}, u32[]{:S(2)}, u32[]{:S(2)}) collective-permute-start(bf16[512,1024]{0,1:T(8,128)(2,1)S(1)} %bitcast.77), channel_id=1, source_target_pairs={{4,0},{8,4},{12,8},{16,12},{20,16},{24,20},{28,24},{0,28},{5,1},{9... | collective-permute-start | bytes 3145736 | tf_op jit(solution)/shard_map/ppermute | solution.py:13
  50.0 1.1 bitcast_dynamic-update-slice_fusion.5
  51.1 0.0 collective-permute-done.3
  51.2 0.0 copy-start.2
  51.2 1.5 copy-done.2
  52.6 41.2 %collective-permute-done.4 = bf16[512,1024]{0,1:T(8,128)(2,1)S(1)} collective-permute-done((bf16[512,1024]{0,1:T(8,128)(2,1)S(1)}, bf16[512,1024]{0,1:T(8,128)(2,1)S(1)}, u32[]{:S(2)}, u32[]{:S(2)}) %collective-permute-start.4) | collective-permute-done | bytes 1048608 | tf_op jit(solution)/shard_map/ppermute | solution.py:13
  93.8 0.1 bitcast_dynamic-update-slice_fusion.3
  93.9 20.8 %collective-permute-done.5 = bf16[512,1024]{0,1:T(8,128)(2,1)S(1)} collective-permute-done((bf16[512,1024]{0,1:T(8,128)(2,1)S(1)}, bf16[512,1024]{0,1:T(8,128)(2,1)S(1)}, u32[]{:S(2)}, u32[]{:S(2)}) %collective-permute-start.5) | collective-permute-done | bytes 1048608 | tf_op jit(solution)/shard_map/ppermute | solution.py:13
  114.7 0.1 bitcast_dynamic-update-slice_fusion.2
  114.8 0.1 constant_dynamic-update-slice_fusion.1
  114.8 0.0 collective-permute-done.6
  114.9 0.1 bitcast_dynamic-update-slice_fusion.1
  114.9 0.0 collective-permute-done.7
  114.9 0.1 bitcast_dynamic-update-slice_fusion
  115.0 0.0 copy-start.1
  115.0 0.1 broadcast_in_dim.6
  115.2 2.3 copy-done.1
  117.4 29.3 %while.14 = (s32[]{:T(128)}, f32[256,1024]{1,0:T(8,128)S(1)}, s32[]{:T(128)}, s32[4,3]{1,0:T(4,128)S(1)}, bf16[5,256,1024]{2,1,0:T(8,128)(2,1)}, /*index=5*/bf16...) while((s32[]{:T(128)}, f32[256,1024]{1,0:T(8,128)S(1)}, s32[]{:T(128)}, ...), condition=%wide.region_1.2_spmd, body=%wide.region_0.1_spmd.sunk | while | flops 1611923456 | bytes 17301812 | solution.py:39
  118.1 0.7 fusion.16
  124.2 1.7 constant_dynamic-slice_fusion.6
  125.9 7.0 %convert_bitcast_fusion.2 = bf16[32,32,32,32]{1,0,3,2:T(8,128)(2,1)} fusion(bf16[32,32,512,1]{2,1,3,0:T(8,128)(2,1)S(1)} %bitcast.73, bf16[32,32,512,1]{2,1,0,3:T(8,128)(2,1)S(1)} %bitcast.72), kind=kOutput, calls=%fused_computation.clone.1 | convolution fusion | flops 1074790400 | bytes 4194304 | tf_op jit(solution)/shard_map/while/body/dot_general | solution.py:17
  132.8 11.3 %convert_element_type.19 = bf16[1024,1024]{0,1:T(8,128)(2,1)S(1)} reshape(bf16[32,32,32,32]{1,0,3,2:T(8,128)(2,1)} %convert_bitcast_fusion.2) | data formatting | bytes 4194304 | tf_op jit(solution)/shard_map/while/body/convert_element_type | solution.py:25
  144.2 1.9 convolution_add_fusion.2
  146.7 0.0 copy-start
  146.8 1.0 copy-done
  147.7 0.0 reduce-scatter.2.cloned.1.call-update
  147.8 107.3 %reduce-scatter.2.cloned.1.call-done = f32[256,256]{1,0:T(8,128)} async-done(((f32[256,1024]{1,0:T(8,128)}), f32[256,256]{1,0:T(8,128)}) %reduce-scatter.2.cloned.1.call-update) | async-done | bytes 262160 | tf_op jit(solution)/shard_map/reduce_scatter | solution.py:61
  (3 shorter events, 0.1 us)
Async XLA Ops:
  6.5 31.7 %copy-start.3 = (bf16[1,256,1024]{2,1,0:T(8,128)(2,1)S(1)}, bf16[1,256,1024]{2,1,0:T(8,128)(2,1)}, u32[]{:S(2)}) copy-start(bf16[1,256,1024]{2,1,0:T(8,128)(2,1)} %param.7) | copy-start | bytes 1572868
  6.5 248.5 %reduce-scatter.2.cloned.1.call-start = ((), (), s32[]{:S(2)}) async-start(), calls=%async_computation.1 | async-start | bytes 1310720 | tf_op jit(solution)/shard_map/reduce_scatter | solution.py:61
  6.5 18.3 %collective-permute-start = (bf16[256,1024]{1,0:T(8,128)(2,1)}, bf16[256,1024]{1,0:T(8,128)(2,1)}, u32[]{:S(2)}, u32[]{:S(2)}) collective-permute-start(bf16[256,1024]{1,0:T(8,128)(2,1)} %bitcast.78), channel_id=1, source_target_pairs={{24,0},{28,4},{0,8},{4,12},{8,16},{12,20},{16,24},{20,28},{25,1},{... | collective-permute-start | bytes 1572872 | tf_op jit(solution)/shard_map/ppermute | solution.py:13
  9.6 27.6 %collective-permute-start.1 = (bf16[256,1024]{1,0:T(8,128)(2,1)}, bf16[256,1024]{1,0:T(8,128)(2,1)}, u32[]{:S(2)}, u32[]{:S(2)}) collective-permute-start(bf16[256,1024]{1,0:T(8,128)(2,1)} %bitcast.79), channel_id=1, source_target_pairs={{28,0},{0,4},{4,8},{8,12},{12,16},{16,20},{20,24},{24,28},{29,1},{... | collective-permute-start | bytes 1572872 | tf_op jit(solution)/shard_map/ppermute | solution.py:13
  11.1 40.0 %collective-permute-start.3 = (bf16[256,1024]{1,0:T(8,128)(2,1)}, bf16[256,1024]{1,0:T(8,128)(2,1)S(1)}, u32[]{:S(2)}, u32[]{:S(2)}) collective-permute-start(bf16[256,1024]{1,0:T(8,128)(2,1)} %bitcast.80), channel_id=1, source_target_pairs={{8,0},{12,4},{16,8},{20,12},{24,16},{28,20},{0,24},{4,28},{9,1},{1... | collective-permute-start | bytes 1572872 | tf_op jit(solution)/shard_map/ppermute | solution.py:13
  13.4 31.4 %collective-permute-start.2 = (bf16[256,1024]{1,0:T(8,128)(2,1)}, bf16[256,1024]{1,0:T(8,128)(2,1)}, u32[]{:S(2)}, u32[]{:S(2)}) collective-permute-start(bf16[256,1024]{1,0:T(8,128)(2,1)} %bitcast.81), channel_id=1, source_target_pairs={{4,0},{8,4},{12,8},{16,12},{20,16},{24,20},{28,24},{0,28},{5,1},{9... | collective-permute-start | bytes 1572872 | tf_op jit(solution)/shard_map/ppermute | solution.py:13
  16.1 98.8 %collective-permute-start.7 = (bf16[512,1024]{0,1:T(8,128)(2,1)S(1)}, bf16[512,1024]{0,1:T(8,128)(2,1)S(1)}, u32[]{:S(2)}, u32[]{:S(2)}) collective-permute-start(bf16[512,1024]{0,1:T(8,128)(2,1)S(1)} %bitcast.74), channel_id=1, source_target_pairs={{8,0},{12,4},{16,8},{20,12},{24,16},{28,20},{0,24},{4,28},{9,1},{1... | collective-permute-start | bytes 3145736 | tf_op jit(solution)/shard_map/ppermute | solution.py:13
  24.8 69.0 %collective-permute-start.4 = (bf16[512,1024]{0,1:T(8,128)(2,1)S(1)}, bf16[512,1024]{0,1:T(8,128)(2,1)S(1)}, u32[]{:S(2)}, u32[]{:S(2)}) collective-permute-start(bf16[512,1024]{0,1:T(8,128)(2,1)S(1)} %bitcast.75), channel_id=1, source_target_pairs={{24,0},{28,4},{0,8},{4,12},{8,16},{12,20},{16,24},{20,28},{25,1},{... | collective-permute-start | bytes 3145736 | tf_op jit(solution)/shard_map/ppermute | solution.py:13
  37.2 77.5 %collective-permute-start.5 = (bf16[512,1024]{0,1:T(8,128)(2,1)S(1)}, bf16[512,1024]{0,1:T(8,128)(2,1)S(1)}, u32[]{:S(2)}, u32[]{:S(2)}) collective-permute-start(bf16[512,1024]{0,1:T(8,128)(2,1)S(1)} %bitcast.76), channel_id=1, source_target_pairs={{28,0},{0,4},{4,8},{8,12},{12,16},{16,20},{20,24},{24,28},{29,1},{... | collective-permute-start | bytes 3145736 | tf_op jit(solution)/shard_map/ppermute | solution.py:13
  44.7 70.1 %collective-permute-start.6 = (bf16[512,1024]{0,1:T(8,128)(2,1)S(1)}, bf16[512,1024]{0,1:T(8,128)(2,1)S(1)}, u32[]{:S(2)}, u32[]{:S(2)}) collective-permute-start(bf16[512,1024]{0,1:T(8,128)(2,1)S(1)} %bitcast.77), channel_id=1, source_target_pairs={{4,0},{8,4},{12,8},{16,12},{20,16},{24,20},{28,24},{0,28},{5,1},{9... | collective-permute-start | bytes 3145736 | tf_op jit(solution)/shard_map/ppermute | solution.py:13
  51.2 1.5 copy-start.2
  115.0 2.4 copy-start.1
  146.7 1.0 copy-start
Sparse Core Ops, SparseCore 0:
  147.9 107.0 reduce-scatter.1
where the time goes:
time: 264 us; the launch traced here: 262 us
  waiting for transfers between devices  193 us (73%)
  local copies, waits for them, and re-layouts  24.4 us (9%)
  starting transfers between devices  15.4 us (6%)
  between operations  13.5 us (5%)
  matrix products  8.89 us (3%)
  loops' own time  6.74 us (3%)
    reduce_scatter x1, waiting for transfers between devices, shards(): lax.psum_scatter(partial_sum, 'aux', scatter_dimension=1, tiled=True)  107 us
    ppermute x8, waiting for transfers between devices, shifted(): return lax.ppermute(block, axis, route)  85.6 us
    ppermute x8, starting transfers between devices, shifted(): return lax.ppermute(block, axis, route)  15.4 us
    convert_element_type x1, local copies, waits for them, and re-layouts, task_term(): tile = tile.astype(jnp.bfloat16)  11.3 us
    unnamed x18, local copies, waits for them, and re-layouts  10.5 us
    dot_general x1, matrix products, task_term(): lax.dot_general(first, second, (((0,), (0,)), ((), ())), preferred_elemen...  6.97 us
    another operation x1, loops' own time, run_tasks(): return lax.fori_loop(first, last, one_task, start)  6.74 us
  transfers between devices with their start and end apart: 9, of which 6 were waited for; matrix products, arithmetic and copies ran while one was open for 2% of the time, Pallas kernels for 0%

commit v1 on v0

v1 whole, which is shorter than its diff:
```python
import jax
import jax.numpy as jnp
from jax import lax
from jax.experimental import pallas as pl
from jax.experimental.pallas import tpu as pltpu
from jax.sharding import PartitionSpec as P

VB = 32
RADIUS = 2
SPAN = 2 * RADIUS + 1
LANES = 128
SPREAD = LANES // VB
STEP = 2


def shifted(block, axis, distance):
    devices = range(lax.axis_size(axis))
    route = [((i - distance) % len(devices), i) for i in devices]
    return lax.ppermute(block, axis, route)


def swap_matrix(width):
    pairs = width * width
    rows = lax.broadcasted_iota(jnp.int32, (pairs, pairs), 0)
    cols = lax.broadcasted_iota(jnp.int32, (pairs, pairs), 1)
    return (rows == (cols % width) * width + cols // width).astype(jnp.bfloat16)


def roll_groups(x, amount):
    if amount == 0:
        return x
    parts = [
        pltpu.roll(x[:, j * LANES : (j + 1) * LANES], amount, 1)
        for j in range(x.shape[1] // LANES)
    ]
    return jnp.concatenate(parts, axis=1)


def kernel(counts, plan, swap, *refs):
    fac_in, amp_in = refs[:SPAN], refs[SPAN : 2 * SPAN]
    out, fac, amp, flip, tile, sems = refs[2 * SPAN :]
    pairs = swap.shape[0]
    blocks = pairs // LANES
    copies = [pltpu.make_async_copy(fac_in[i], fac.at[i], sems.at[i]) for i in range(SPAN)]
    copies += [
        pltpu.make_async_copy(amp_in[i], amp.at[i], sems.at[SPAN + i]) for i in range(SPAN)
    ]
    for copy in copies:
        copy.start()
    out[...] = jnp.zeros_like(out)
    for copy in copies:
        copy.wait()
    lanes = STEP * LANES
    group = (lax.broadcasted_iota(jnp.int32, (VB * blocks, lanes), 1) // VB) % SPREAD

    @pl.loop(0, counts[0])
    def _(slot):
        left, right, third = plan[slot, 0], plan[slot, 1], plan[slot, 2]
        for a_hi in range(blocks):
            strip = fac[left, :, a_hi * LANES : (a_hi + 1) * LANES].T
            for s in range(SPREAD):
                flip[s, a_hi * VB : (a_hi + 1) * VB, :] = strip[s * VB : (s + 1) * VB, :]

        @pl.loop(0, blocks // STEP)
        def _(step):
            base = pl.multiple_of(step * lanes, lanes)
            cols = swap[:, pl.ds(base, lanes)]
            swapped = jnp.dot(fac[right], cols, preferred_element_type=jnp.float32)
            outs = []
            for s in range(SPREAD):
                turned = roll_groups(swapped, s * VB).astype(jnp.bfloat16)
                outs.append(jnp.dot(flip[s], turned, preferred_element_type=jnp.float32))
            for t in range(SPREAD):
                mixed = outs[(SPREAD - 1 - t) % SPREAD]
                for g in range(SPREAD - 1):
                    mixed = jnp.where(group == g, outs[(g - t) % SPREAD], mixed)
                mixed = roll_groups(mixed, (LANES - t * VB) % LANES).astype(jnp.bfloat16)
                for j in range(STEP):
                    row = pl.multiple_of(base + (j * SPREAD + t) * VB, VB)
                    for a_hi in range(blocks):
                        tile[pl.ds(row, VB), a_hi * LANES : (a_hi + 1) * LANES] = mixed[
                            a_hi * VB : (a_hi + 1) * VB, j * LANES : (j + 1) * LANES
                        ]

        @pl.loop(0, blocks // STEP)
        def _(step):
            base = pl.multiple_of(step * lanes, lanes)
            amps = jnp.dot(
                amp[third], swap[:, pl.ds(base, lanes)], preferred_element_type=jnp.float32
            ).astype(jnp.bfloat16)
            out[...] += jnp.dot(
                amps, tile[pl.ds(base, lanes), :], preferred_element_type=jnp.float32
            )


def run_tasks(facs, amps, counts, plan):
    depth, pairs = facs[0].shape
    occ = amps[0].shape[0]
    anywhere = pl.BlockSpec(memory_space=pl.ANY)
    scalars = pl.BlockSpec(memory_space=pltpu.SMEM)
    return pl.pallas_call(
        kernel,
        out_shape=jax.ShapeDtypeStruct((occ, pairs), jnp.float32),
        in_specs=[scalars, scalars, pl.BlockSpec(memory_space=pltpu.VMEM)]
        + [anywhere] * (2 * SPAN),
        out_specs=pl.BlockSpec(memory_space=pltpu.VMEM),
        scratch_shapes=[
            pltpu.VMEM((SPAN, depth, pairs), jnp.bfloat16),
            pltpu.VMEM((SPAN, occ, pairs), jnp.bfloat16),
            pltpu.VMEM((SPREAD, pairs // SPREAD, depth), jnp.bfloat16),
            pltpu.VMEM((pairs, pairs), jnp.bfloat16),
            pltpu.SemaphoreType.DMA((2 * SPAN,)),
        ],
        compiler_params=pltpu.CompilerParams(vmem_limit_bytes=48 * 1024 * 1024),
    )(counts, plan, swap_matrix(VB), *facs, *amps)


def shards(factors, amplitudes, task_counts, task_tiles):
    own_fac = factors[0]
    own_amp = amplitudes[0]
    facs = []
    amps = []
    for offset in range(-RADIUS, RADIUS + 1):
        if offset == 0:
            facs.append(own_fac)
            amps.append(own_amp)
        else:
            moved = shifted((own_fac, own_amp), "task", -offset)
            facs.append(moved[0])
            amps.append(moved[1])
    partial_sum = run_tasks(facs, amps, task_counts, task_tiles[0])
    summed = lax.psum_scatter(partial_sum, "aux", scatter_dimension=1, tiled=True)
    return summed[None]


def solution(mesh):
    return jax.shard_map(
        shards,
        mesh=mesh,
        in_specs=(P("task", "aux", None), P("task", None, None), P("task"), P("task", None, None)),
        out_specs=P("task", None, "aux"),
        check_vma=False,
    )
```

time: 264 us -> 186 us (0.70)
  waiting for transfers between devices: 193 us -> 132 us
  Pallas kernels: 0 us -> 23.2 us
  local copies, waits for them, and re-layouts: 24.4 us -> 1.58 us
  matrix products: 8.89 us -> 0 us
  loops' own time: 6.74 us -> 0 us
    reduce_scatter x1, waiting for transfers between devices: 107 us -> 41.5 us  [shards(): lax.psum_scatter(partial_sum, 'aux', scatter_dimension=1, tiled=True)]
    pallas_call x0 -> x1, Pallas kernels: none -> 23.2 us  [run_tasks(): pl.pallas_call(kernel, out_shape=jax.ShapeDtypeStruct((occ, pairs), jnp.f...]
    convert_element_type x1 -> x0, local copies, waits for them, and re-layouts: 11.3 us -> none  [task_term(): tile = tile.astype(jnp.bfloat16)]
    unnamed x18 -> x7, local copies, waits for them, and re-layouts: 10.5 us -> 1.58 us
    dot_general x2 -> x0, matrix products: 8.89 us -> none  [the longest x1 6.97 us: task_term(): lax.dot_general(first, second, (((0,), (0,)), ((), ())), preferred_elemen...]
    another operation x1 -> x0, loops' own time: 6.74 us -> none  [run_tasks(): return lax.fori_loop(first, last, one_task, start)]
    ppermute x8, waiting for transfers between devices: 85.6 us -> 90.2 us  [shifted(): return lax.ppermute(block, axis, route)]
  transfers between devices with their start and end apart: 9 -> 9, of which waited for: 6 -> 4; matrix products, arithmetic and copies ran while one was open for 2% -> 2% of each run, Pallas kernels for 0% -> 0%
where the time goes in v1:
time: 186 us
  waiting for transfers between devices  132 us (71%)
  Pallas kernels  23.2 us (12%)
  between operations  14.1 us (8%)
  starting transfers between devices  12.8 us (7%)
  other arithmetic  2.09 us (1%)
    ppermute x8, waiting for transfers between devices, shifted(): return lax.ppermute(block, axis, route)  90.2 us
    reduce_scatter x1, waiting for transfers between devices, shards(): lax.psum_scatter(partial_sum, 'aux', scatter_dimension=1, tiled=True)  41.5 us
    pallas_call x1, Pallas kernels, run_tasks(): pl.pallas_call(kernel, out_shape=jax.ShapeDtypeStruct((occ, pairs), jnp.f...  23.2 us
    ppermute x8, starting transfers between devices, shifted(): return lax.ppermute(block, axis, route)  12.8 us
  transfers between devices with their start and end apart: 9, of which 4 were waited for; matrix products, arithmetic and copies ran while one was open for 2% of the time, Pallas kernels for 0%

profile of v1, /device:TPU:0, one launch (start us, length us, event | category | flops | bytes accessed | tf_op | source)
XLA Modules:
  0.0 185.5 jit_solution(13917026145621492430)
XLA Ops:
  6.5 0.0 copy-start
  6.5 0.0 reduce-scatter.2.cloned.1.call-start
  6.5 5.1 %collective-permute-start.7 = (bf16[256,1024]{1,0:T(8,128)(2,1)}, bf16[256,1024]{1,0:T(8,128)(2,1)S(1)}, u32[]{:S(2)}, u32[]{:S(2)}) collective-permute-start(bf16[256,1024]{1,0:T(8,128)(2,1)} %bitcast.4), channel_id=1, source_target_pairs={{8,0},{12,4},{16,8},{20,12},{24,16},{28,20},{0,24},{4,28},{9,1},{1... | collective-permute-start | bytes 1572872 | tf_op jit(solution)/shard_map/ppermute | solution.py:19
  11.6 1.4 collective-permute-start.6
  13.0 0.6 collective-permute-start.5
  13.6 0.4 collective-permute-start.3
  14.1 3.7 %collective-permute-start.2 = (bf16[512,1024]{1,0:T(8,128)(2,1)}, bf16[512,1024]{1,0:T(8,128)(2,1)}, u32[]{:S(2)}, u32[]{:S(2)}) collective-permute-start(bf16[512,1024]{1,0:T(8,128)(2,1)} %bitcast.11), channel_id=1, source_target_pairs={{4,0},{8,4},{12,8},{16,12},{20,16},{24,20},{28,24},{0,28},{5,1},{9... | collective-permute-start | bytes 3145736 | tf_op jit(solution)/shard_map/ppermute | solution.py:19
  17.8 6.5 %collective-permute-done.7.refs_9_ = bf16[256,1024]{1,0:T(8,128)(2,1)S(1)} collective-permute-done((bf16[256,1024]{1,0:T(8,128)(2,1)}, bf16[256,1024]{1,0:T(8,128)(2,1)S(1)}, u32[]{:S(2)}, u32[]{:S(2)}) %collective-permute-start.7) | collective-permute-done | bytes 524320 | tf_op jit(solution)/shard_map/ppermute | solution.py:19
  24.2 1.5 collective-permute-start.1
  25.8 12.1 %collective-permute-done.6.refs_8_ = bf16[256,1024]{1,0:T(8,128)(2,1)S(1)} collective-permute-done((bf16[256,1024]{1,0:T(8,128)(2,1)}, bf16[256,1024]{1,0:T(8,128)(2,1)S(1)}, u32[]{:S(2)}, u32[]{:S(2)}) %collective-permute-start.6) | collective-permute-done | bytes 524320 | tf_op jit(solution)/shard_map/ppermute | solution.py:19
  37.9 0.0 copy-start.1
  37.9 0.8 copy-done.1
  38.7 0.0 collective-permute-start
  39.3 0.8 copy.5
  40.1 0.0 copy-start.2
  40.1 0.0 collective-permute-done.5.refs_6_
  40.1 0.1 collective-permute-start.4
  40.2 2.1 %fusion.swap = bf16[1024,1024]{1,0:T(8,128)(2,1)} fusion(s32[1024]{0:T(1024)S(1)} %get-tuple-element.5, s32[1024]{0:T(1024)S(1)} %get-tuple-element.8, s32[1024]{0:T(1024)S(1)} %get-tuple-element.6, s32[1024]{0:T(1024)S(1)} %get-tuple-element.7, pred[1024]{0:T(1024)(128)(4,1)S(1)} %get-tuple-element.9, pred[1024]{0:T(1024)(128)(4,1)S(1)} %get-tuple-element.10), kind=kLoop, calls=%fused_computation.1 | loop fusion | flops 6291456 | bytes 2115584 | tf_op jit(solution)/shard_map/convert_element_type | solution.py:26
  42.3 71.6 %collective-permute-done.4.refs_5_ = bf16[256,1024]{1,0:T(8,128)(2,1)S(1)} collective-permute-done((bf16[256,1024]{1,0:T(8,128)(2,1)}, bf16[256,1024]{1,0:T(8,128)(2,1)S(1)}, u32[]{:S(2)}, u32[]{:S(2)}) %collective-permute-start.4) | collective-permute-done | bytes 524320 | tf_op jit(solution)/shard_map/ppermute | solution.py:19
  113.9 0.0 collective-permute-done.3.refs_4_
  113.9 0.0 collective-permute-done.2.refs_3_
  113.9 0.0 collective-permute-done.1.refs_1_
  113.9 0.0 collective-permute-done.refs_0_
  113.9 0.0 copy-done
  113.9 0.0 copy-done.2
  113.9 23.2 %shard_map.46 = f32[256,1024]{1,0:T(8,128)} custom-call(s32[1]{0:T(128)S(6)} %copy.6.counts, s32[4,3]{1,0:T(4,128)S(1)} %bitcast.9, bf16[1024,1024]{1,0:T(8,128)(2,1)} %fusion.swap, bf16[512,1024]{1,0:T(8,128)(2,1)S(1)} %collective-permute-done.refs_0_, bf16[512,1024]{1,0:T(8,128)(2,1)S(1)} %collective-permute-done.1.refs_1_, bf16[512,1024]{1,0:T(8,128)(2,1)} %bitcast.14, ...), custom_call_target="tpu_custom_call" | custom-call | tf_op jit(solution)/shard_map/pallas_call | solution.py:101
  137.2 0.0 reduce-scatter.2.cloned.1.call-update
  137.2 41.5 %reduce-scatter.2.cloned.1.call-done = f32[256,256]{1,0:T(8,128)} async-done(((f32[256,1024]{1,0:T(8,128)}), f32[256,256]{1,0:T(8,128)}) %reduce-scatter.2.cloned.1.call-update) | async-done | bytes 262160 | tf_op jit(solution)/shard_map/reduce_scatter | solution.py:132
  (3 shorter events, 0.0 us)
Async XLA Ops:
  6.5 107.4 %copy-start = (bf16[1,256,1024]{2,1,0:T(8,128)(2,1)S(1)}, bf16[1,256,1024]{2,1,0:T(8,128)(2,1)}, u32[]{:S(2)}) copy-start(bf16[1,256,1024]{2,1,0:T(8,128)(2,1)} %param.5) | copy-start | bytes 1572868
  6.5 172.2 %reduce-scatter.2.cloned.1.call-start = ((), (), s32[]{:S(2)}) async-start(), calls=%async_computation.1 | async-start | bytes 1310720 | tf_op jit(solution)/shard_map/reduce_scatter | solution.py:132
  6.5 17.7 %collective-permute-start.7 = (bf16[256,1024]{1,0:T(8,128)(2,1)}, bf16[256,1024]{1,0:T(8,128)(2,1)S(1)}, u32[]{:S(2)}, u32[]{:S(2)}) collective-permute-start(bf16[256,1024]{1,0:T(8,128)(2,1)} %bitcast.4), channel_id=1, source_target_pairs={{8,0},{12,4},{16,8},{20,12},{24,16},{28,20},{0,24},{4,28},{9,1},{1... | collective-permute-start | bytes 1572872 | tf_op jit(solution)/shard_map/ppermute | solution.py:19
  11.6 26.2 %collective-permute-start.6 = (bf16[256,1024]{1,0:T(8,128)(2,1)}, bf16[256,1024]{1,0:T(8,128)(2,1)S(1)}, u32[]{:S(2)}, u32[]{:S(2)}) collective-permute-start(bf16[256,1024]{1,0:T(8,128)(2,1)} %bitcast.5), channel_id=1, source_target_pairs={{4,0},{8,4},{12,8},{16,12},{20,16},{24,20},{28,24},{0,28},{5,1},{9... | collective-permute-start | bytes 1572872 | tf_op jit(solution)/shard_map/ppermute | solution.py:19
  13.0 27.1 %collective-permute-start.5 = (bf16[256,1024]{1,0:T(8,128)(2,1)}, bf16[256,1024]{1,0:T(8,128)(2,1)}, u32[]{:S(2)}, u32[]{:S(2)}) collective-permute-start(bf16[256,1024]{1,0:T(8,128)(2,1)} %bitcast.6), channel_id=1, source_target_pairs={{28,0},{0,4},{4,8},{8,12},{12,16},{16,20},{20,24},{24,28},{29,1},{... | collective-permute-start | bytes 1572872 | tf_op jit(solution)/shard_map/ppermute | solution.py:19
  13.6 100.2 %collective-permute-start.3 = (bf16[512,1024]{1,0:T(8,128)(2,1)}, bf16[512,1024]{1,0:T(8,128)(2,1)}, u32[]{:S(2)}, u32[]{:S(2)}) collective-permute-start(bf16[512,1024]{1,0:T(8,128)(2,1)} %bitcast.10), channel_id=1, source_target_pairs={{8,0},{12,4},{16,8},{20,12},{24,16},{28,20},{0,24},{4,28},{9,1},{1... | collective-permute-start | bytes 3145736 | tf_op jit(solution)/shard_map/ppermute | solution.py:19
  14.1 99.8 %collective-permute-start.2 = (bf16[512,1024]{1,0:T(8,128)(2,1)}, bf16[512,1024]{1,0:T(8,128)(2,1)}, u32[]{:S(2)}, u32[]{:S(2)}) collective-permute-start(bf16[512,1024]{1,0:T(8,128)(2,1)} %bitcast.11), channel_id=1, source_target_pairs={{4,0},{8,4},{12,8},{16,12},{20,16},{24,20},{28,24},{0,28},{5,1},{9... | collective-permute-start | bytes 3145736 | tf_op jit(solution)/shard_map/ppermute | solution.py:19
  24.2 89.7 %collective-permute-start.1 = (bf16[512,1024]{1,0:T(8,128)(2,1)}, bf16[512,1024]{1,0:T(8,128)(2,1)S(1)}, u32[]{:S(2)}, u32[]{:S(2)}) collective-permute-start(bf16[512,1024]{1,0:T(8,128)(2,1)} %bitcast.12), channel_id=1, source_target_pairs={{28,0},{0,4},{4,8},{8,12},{12,16},{16,20},{20,24},{24,28},{29,1},{... | collective-permute-start | bytes 3145736 | tf_op jit(solution)/shard_map/ppermute | solution.py:19
  37.9 0.8 copy-start.1
  38.7 75.2 %collective-permute-start = (bf16[512,1024]{1,0:T(8,128)(2,1)}, bf16[512,1024]{1,0:T(8,128)(2,1)S(1)}, u32[]{:S(2)}, u32[]{:S(2)}) collective-permute-start(bf16[512,1024]{1,0:T(8,128)(2,1)} %bitcast.13), channel_id=1, source_target_pairs={{24,0},{28,4},{0,8},{4,12},{8,16},{12,20},{16,24},{20,28},{25,1},{... | collective-permute-start | bytes 3145736 | tf_op jit(solution)/shard_map/ppermute | solution.py:19
  40.1 73.8 %copy-start.2 = (bf16[256,1024]{1,0:T(8,128)(2,1)S(1)}, bf16[256,1024]{1,0:T(8,128)(2,1)}, u32[]{:S(2)}) copy-start(bf16[256,1024]{1,0:T(8,128)(2,1)} %copy-done.1) | copy-start | bytes 1572868
  40.1 73.8 %collective-permute-start.4 = (bf16[256,1024]{1,0:T(8,128)(2,1)}, bf16[256,1024]{1,0:T(8,128)(2,1)S(1)}, u32[]{:S(2)}, u32[]{:S(2)}) collective-permute-start(bf16[256,1024]{1,0:T(8,128)(2,1)} %bitcast.7), channel_id=1, source_target_pairs={{24,0},{28,4},{0,8},{4,12},{8,16},{12,20},{16,24},{20,28},{25,1},{... | collective-permute-start | bytes 1572872 | tf_op jit(solution)/shard_map/ppermute | solution.py:19
Sparse Core Ops, SparseCore 0:
  137.3 41.3 reduce-scatter.1
